TPU v7x, 32 devices: a whole 2x2x4 slice. The times are simulated.
32 devices in a mesh: win: 8 (over z, x), fsdp: 4 (over y, core).
Axes of the slice: x: 2, y: 2, z: 4, core: 2. Of those that a mesh axis runs over, the one named last changes fastest.
Arguments:
- queries: bfloat16 [8192, 2560], P(('win', 'fsdp')), may hold values from -5 to 5
- keys: bfloat16 [8192, 2560], P(('win', 'fsdp')), may hold values from -5 to 5
- values: bfloat16 [8192, 2560], P(('win', 'fsdp')), may hold values from -6 to 6
- stream: bfloat16 [8192, 5120], P(('win', 'fsdp')), may hold values from -0.59765625 to 0.59765625
- out_weight: bfloat16 [2560, 5120], P('fsdp', 'win'), may hold values from -0.125 to 0.125
- gate: float32 [5120], replicated, may hold values from 0.5 to 2
- head_shift: float32 [5120], replicated, may hold values from -3 to 3
- head_scale: float32 [5120], replicated, may hold values from 0.25 to 1.75
- head_weight: bfloat16 [5120, 64], replicated, may hold values from -0.078125 to 0.078125
- latents: float32 [128, 4096], P('win', 'fsdp'), may hold values from -6 to 6
- step_size: float32 [1], replicated, may hold values from 0.5 to 1
- intersections: int32 [8], replicated, may hold values from 1 to 4
- ramps: int32 [8, 4, 2], replicated, may hold values from 1 to 16
Outputs:
- blended: float32 [128, 4096], P('win', 'fsdp')
All inputs are finite; a program needn't handle non-finite values.
Results may differ from a plain program's by a relative error of at most 0.0065.
Values may be sent and summed in bfloat16 or wider, within the bound.
A program may use at most 128 MiB of HBM per device.

v0:
```python
import math
import jax
import jax.numpy as jnp
from jax import lax
from jax.sharding import PartitionSpec as P

HEADS = 20
HD = 128
FD = 4
EPSILON = 0.001


def padded_2(value, sides, width):
    for axis, dim in sides:
        size, length = (lax.axis_size(axis), value.shape[dim])
        up = [(i, (i + 1) % size) for i in range(size)]
        down = [(j, i) for i, j in up]
        last = lax.slice_in_dim(value, length - width, length, axis=dim)
        initial = lax.slice_in_dim(value, 0, width, axis=dim)
        before = lax.ppermute(last, axis, up)
        after = lax.ppermute(initial, axis, down)
        value = jnp.concatenate([before, value, after], axis=dim)
    return value


def softmax_block(query_h, key_h, value_h, score_scale):
    scores = (
        jnp.einsum("qhd,khd->hqk", query_h, key_h, preferred_element_type=jnp.float32) * score_scale
    )
    highest = jnp.max(scores, axis=-1, keepdims=True)
    exponent = jnp.exp(scores - highest)
    denominator = jnp.sum(exponent, axis=-1)
    probability = exponent.astype(jnp.bfloat16)
    summed = jnp.einsum("hqk,khd->qhd", probability, value_h, preferred_element_type=jnp.float32)
    return summed / jnp.transpose(denominator)[:, :, None]


def local(
    queries,
    keys,
    values,
    stream,
    out_weight,
    gate,
    head_shift,
    head_scale,
    head_weight,
    latents,
    step_size,
    intersections,
    ramps,
):
    tok_rows, feat_width = queries.shape
    groups = lax.axis_size("fsdp")
    head_count = HEADS
    score_scale = 1.0 / math.sqrt(HD)
    per_group = head_count // groups
    split_shape = (tok_rows, groups, per_group, HD)
    query_part = lax.all_to_all(
        queries.reshape(split_shape), "fsdp", split_axis=1, concat_axis=0, tiled=True
    )
    key_part = lax.all_to_all(
        keys.reshape(split_shape), "fsdp", split_axis=1, concat_axis=0, tiled=True
    )
    value_part = lax.all_to_all(
        values.reshape(split_shape), "fsdp", split_axis=1, concat_axis=0, tiled=True
    )
    result = softmax_block(query_part[:, 0], key_part[:, 0], value_part[:, 0], score_scale)
    own_heads = result.astype(jnp.bfloat16)[:, None]
    window_rows = own_heads.shape[0]
    own_heads = own_heads.reshape(window_rows, per_group * HD)
    full_columns = lax.all_gather(out_weight, "win", axis=1, tiled=True)
    projected = lax.psum_scatter(
        jnp.dot(own_heads, full_columns, preferred_element_type=jnp.float32).astype(jnp.bfloat16),
        "fsdp",
        scatter_dimension=0,
        tiled=True,
    ).astype(jnp.float32)
    hidden = stream.astype(jnp.float32) + gate * projected
    centre = jnp.mean(hidden, axis=-1, keepdims=True)
    centred = hidden - centre
    variance = jnp.mean(centred * centred, axis=-1, keepdims=True)
    normed = centred / jnp.sqrt(variance + EPSILON)
    modulated = (normed * head_scale + head_shift).astype(jnp.bfloat16)
    velocity = jnp.dot(modulated, head_weight, preferred_element_type=jnp.float32)
    fresh = latents + step_size[0] * velocity.reshape(latents.shape)
    frames_dev = latents.shape[0]
    shared = FD
    padded = padded_2(fresh.astype(jnp.bfloat16), (("win", 0),), shared).astype(fresh.dtype)
    prev_block = padded[:shared]
    next_block = padded[shared + frames_dev :]
    window = lax.axis_index("win")
    win_count = lax.axis_size("win")
    prev_window = (window + win_count - 1) % win_count
    window_ids = jnp.arange(win_count, dtype=jnp.int32)
    over_prev = jnp.sum(jnp.where(window_ids == prev_window, intersections, 0))
    over_next = jnp.sum(jnp.where(window_ids == window, intersections, 0))
    ramp_prev = jnp.sum(
        jnp.where((window_ids == prev_window)[:, None, None], ramps, 0), axis=0
    ).astype(jnp.float32)
    ramp_own = jnp.sum(jnp.where((window_ids == window)[:, None, None], ramps, 0), axis=0).astype(
        jnp.float32
    )
    frame_ids = jnp.arange(frames_dev, dtype=jnp.int32)
    shared_ids = jnp.arange(shared, dtype=jnp.int32)
    inside_prev = frame_ids < over_prev
    select_prev = (
        (shared_ids[None, :] == shared - over_prev + frame_ids[:, None]) & inside_prev[:, None]
    ).astype(jnp.float32)
    prev_aligned = jnp.dot(select_prev, prev_block, precision=lax.Precision.HIGHEST)
    rows_prev = (shared_ids[None, :] == frame_ids[:, None]).astype(jnp.float32)
    ramp_rows_prev = jnp.dot(rows_prev, ramp_prev, precision=lax.Precision.HIGHEST)
    weight_before = ramp_rows_prev[:, 0:1]
    weight_self = ramp_rows_prev[:, 1:2]
    spare_prev = 1.0 - (frame_ids < shared).astype(jnp.float32)[:, None]
    blend_prev = (weight_before * prev_aligned + weight_self * fresh) / (
        weight_before + weight_self + spare_prev
    )
    shifted = frame_ids - (frames_dev - over_next)
    inside_next = shifted >= 0
    select_next = (shared_ids[None, :] == shifted[:, None]).astype(jnp.float32)
    next_aligned = jnp.dot(select_next, next_block, precision=lax.Precision.HIGHEST)
    ramp_rows = jnp.dot(select_next, ramp_own, precision=lax.Precision.HIGHEST)
    weight_mine = ramp_rows[:, 0:1]
    weight_after = ramp_rows[:, 1:2]
    spare = 1.0 - inside_next.astype(jnp.float32)[:, None]
    blend_next = (weight_mine * fresh + weight_after * next_aligned) / (
        weight_mine + weight_after + spare
    )
    return jnp.where(
        inside_prev[:, None], blend_prev, jnp.where(inside_next[:, None], blend_next, fresh)
    )


def solution(mesh):
    in_specs = (
        P(("win", "fsdp"), None),
        P(("win", "fsdp"), None),
        P(("win", "fsdp"), None),
        P(("win", "fsdp"), None),
        P("fsdp", "win"),
        P(),
        P(),
        P(),
        P(),
        P("win", "fsdp"),
        P(),
        P(),
        P(),
    )
    out_specs = P("win", "fsdp")
    return jax.shard_map(local, mesh=mesh, in_specs=in_specs, out_specs=out_specs, check_vma=False)
```

profile of v0, /device:TPU:0, one launch (start us, length us, event | category | flops | bytes accessed | tf_op | source)
XLA Modules:
  0.0 235.3 jit_solution(2147026987415011485)
XLA Ops:
  6.5 0.0 copy-start
  6.5 0.0 all-gather.2.cloned.1.call-start
  6.5 0.7 all-gather.2.cloned.1.call-update
  7.3 2.4 %copy.18 = bf16[256,2560]{0,1:T(8,128)(2,1)} copy(bf16[256,2560]{1,0:T(8,128)(2,1)} %param.13) | data formatting | bytes 2621440 | tf_op args[0]
  9.7 4.3 %all-to-all-start = ((bf16[256,4,5,128]{0,3,2,1:T(8,128)(2,1)}), bf16[256,4,5,128]{0,3,2,1:T(8,128)(2,1)S(1)}, u32[]{:S(2)}, u32[]{:S(2)}) async-start(bf16[256,4,5,128]{0,3,2,1:T(8,128)(2,1)} %bitcast.2), calls=%async_computation | async-start | bytes 2621440 | tf_op jit(solution)/shard_map/all_to_all | solution.py:59
  14.0 1.4 copy.20
  15.4 15.8 %all-to-all-done = bf16[256,4,5,128]{0,3,2,1:T(8,128)(2,1)S(1)} async-done(((bf16[256,4,5,128]{0,3,2,1:T(8,128)(2,1)}), bf16[256,4,5,128]{0,3,2,1:T(8,128)(2,1)S(1)}, u32[]{:S(2)}, u32[]{:S(2)}) %all-to-all-start) | async-done | bytes 1310752 | tf_op jit(solution)/shard_map/all_to_all | solution.py:59
  31.2 3.5 %all-to-all-start.1 = ((bf16[256,4,5,128]{0,3,2,1:T(8,128)(2,1)}), bf16[256,4,5,128]{0,3,2,1:T(8,128)(2,1)S(1)}, u32[]{:S(2)}, u32[]{:S(2)}) async-start(bf16[256,4,5,128]{0,3,2,1:T(8,128)(2,1)} %bitcast.49), calls=%async_computation.1 | async-start | bytes 2621440 | tf_op jit(solution)/shard_map/all_to_all | solution.py:62
  34.7 2.4 %copy.22 = bf16[256,2560]{0,1:T(8,128)(2,1)} copy(bf16[256,2560]{1,0:T(8,128)(2,1)} %param.15) | data formatting | bytes 2621440 | tf_op args[2]
  37.2 14.8 %all-to-all-done.1 = bf16[256,4,5,128]{0,3,2,1:T(8,128)(2,1)S(1)} async-done(((bf16[256,4,5,128]{0,3,2,1:T(8,128)(2,1)}), bf16[256,4,5,128]{0,3,2,1:T(8,128)(2,1)S(1)}, u32[]{:S(2)}, u32[]{:S(2)}) %all-to-all-start.1) | async-done | bytes 1310752 | tf_op jit(solution)/shard_map/all_to_all | solution.py:62
  52.0 4.3 %all-to-all-start.2 = ((bf16[256,4,5,128]{0,3,2,1:T(8,128)(2,1)}), bf16[256,4,5,128]{0,3,2,1:T(8,128)(2,1)}, u32[]{:S(2)}, u32[]{:S(2)}) async-start(bf16[256,4,5,128]{0,3,2,1:T(8,128)(2,1)} %bitcast.48), calls=%async_computation.2 | async-start | bytes 2621440 | tf_op jit(solution)/shard_map/all_to_all | solution.py:65
  56.3 0.0 reduce-scatter.2.cloned.1.call-start
  56.3 0.8 copy.19
  57.1 1.8 copy.21
  58.9 14.7 %all-to-all-done.2 = bf16[256,4,5,128]{0,3,2,1:T(8,128)(2,1)} async-done(((bf16[256,4,5,128]{0,3,2,1:T(8,128)(2,1)}), bf16[256,4,5,128]{0,3,2,1:T(8,128)(2,1)}, u32[]{:S(2)}, u32[]{:S(2)}) %all-to-all-start.2) | async-done | bytes 1310752 | tf_op jit(solution)/shard_map/all_to_all | solution.py:65
  73.6 3.4 %copy.23 = bf16[4,256,1,5,128]{1,0,4,3,2:T(4,128)(2,1)} copy(bf16[4,256,1,5,128]{1,4,3,0,2:T(8,128)(2,1)} %bitcast.12) | data formatting | bytes 2621440 | tf_op jit(solution)/shard_map/all_to_all | solution.py:65
  77.0 3.7 %squeeze.15 = bf16[1024,5,128]{0,2,1:T(8,128)(2,1)} reshape(bf16[4,256,1,5,128]{1,0,4,3,2:T(4,128)(2,1)} %copy.23) | data formatting | bytes 2621440 | tf_op jit(solution)/shard_map/squeeze | solution.py:68
  80.6 2.9 %multiply_reduce_fusion = (f32[5,1024]{1,0:T(8,128)S(1)}, f32[5,1024,1024]{1,2,0:T(8,128)S(1)}) fusion(bf16[1024,5,128]{2,0,1:T(8,128)(2,1)S(1)} %bitcast.44, bf16[1024,5,128]{2,0,1:T(8,128)(2,1)S(1)} %bitcast.45), kind=kOutput, calls=%fused_computation.1 | convolution fusion | flops 1352657920 | bytes 23613440 | tf_op jit(solution)/shard_map/qhd,khd->hqk/dot_general | solution.py:28
  83.5 3.7 %fusion = f32[5,1024]{1,0:T(8,128)S(1)} fusion(f32[5,1024,1024]{1,2,0:T(8,128)S(1)} %get-tuple-element.20, f32[5,1024]{1,0:T(8,128)S(1)} %get-tuple-element.19), kind=kLoop, calls=%fused_computation.2 | loop fusion | flops 15723520 | bytes 21012480 | tf_op jit(solution)/shard_map/reduce_sum | solution.py:32
  87.2 3.7 %copy-done.1 = f32[5,1024,1024]{1,2,0:T(8,128)} copy-done((f32[5,1024,1024]{1,2,0:T(8,128)}, f32[5,1024,1024]{1,2,0:T(8,128)S(1)}, u32[]{:S(2)}) %copy-start.1) | copy-done | bytes 20971544
  91.0 11.2 %fusion.7 = bf16[1024,5,128]{0,2,1:T(8,128)(2,1)S(1)} fusion(bf16[1024,5,128]{0,2,1:T(8,128)(2,1)S(1)} %copy-done.6, f32[5,1024,1024]{1,2,0:T(8,128)} %copy-done.1, f32[5,1024]{1,0:T(8,128)S(1)} %get-tuple-element.19, f32[1024,5]{0,1:T(8,128)S(1)} %bitcast.50), kind=kOutput, calls=%fused_computation.13 | convolution fusion | flops 1359216640 | bytes 23633920 | tf_op jit(solution)/shard_map/hqk,khd->qhd/dot_general | solution.py:34
  102.2 12.1 %all-gather.2.cloned.1.call-done = bf16[640,5120]{1,0:T(8,128)(2,1)} async-done(((bf16[640,640]{1,0:T(8,128)(2,1)}), bf16[640,5120]{1,0:T(8,128)(2,1)}) %all-gather.2.cloned.1.call-update) | async-done | bytes 6553616 | tf_op jit(solution)/shard_map/all_gather | solution.py:72
  114.3 13.8 %convolution_convert_fusion = bf16[1024,5120]{1,0:T(8,128)(2,1)} fusion(bf16[1024,640]{0,1:T(8,128)(2,1)S(1)} %bitcast.51, bf16[640,5120]{1,0:T(8,128)(2,1)} %all-gather.2.cloned.1.call-done), kind=kOutput, calls=%fused_computation.7 | convolution fusion | flops 6716129280 | bytes 18350080 | tf_op jit(solution)/shard_map/dot_general | solution.py:74
  128.1 0.0 reduce-scatter.2.cloned.1.call-update
  128.9 0.0 copy-done.10
  129.0 0.7 select_reduce_fusion.3
  130.9 0.6 iota_compare_fusion.8
  131.6 0.2 select_reduce_fusion.1
  131.8 0.2 fusion.18
  132.0 0.2 fusion.19
  132.2 0.0 copy-start.11
  132.2 0.0 copy-start.12
  132.2 78.6 %reduce-scatter.2.cloned.1.call-done = bf16[256,5120]{1,0:T(8,128)(2,1)} async-done(((bf16[1024,5120]{1,0:T(8,128)(2,1)}), bf16[256,5120]{1,0:T(8,128)(2,1)}) %reduce-scatter.2.cloned.1.call-update) | async-done | bytes 2621456 | tf_op jit(solution)/shard_map/reduce_scatter | solution.py:73
  210.9 0.0 copy-done.2
  210.9 2.8 %fusion.6 = f32[256]{0:T(256)S(1)} fusion(bf16[256,5120]{1,0:T(8,128)(2,1)} %reduce-scatter.2.cloned.1.call-done, bf16[256,5120]{1,0:T(8,128)(2,1)S(1)} %copy-done.2, f32[5120]{0:T(1024)S(1)} %copy-done.7), kind=kLoop, calls=%fused_computation.11 | loop fusion | flops 6553344 | bytes 5264384 | tf_op jit(solution)/shard_map/reduce_sum | solution.py:80
  213.7 1.3 multiply_reduce_fusion.1
  215.0 0.0 copy-done.11
  215.0 0.0 copy-done.12
  215.0 0.0 copy-start.8
  215.1 1.7 fusion.17
  216.7 0.1 copy.25
  216.8 0.1 mul.85
  217.0 4.3 %collective-permute-start.1 = (bf16[4,1024]{1,0:T(4,128)(2,1)S(1)}, bf16[4,1024]{1,0:T(4,128)(2,1)S(1)}, u32[]{:S(2)}, u32[]{:S(2)}) collective-permute-start(bf16[4,1024]{1,0:T(4,128)(2,1)S(1)} %get-tuple-element.12), channel_id=1, source_target_pairs={{4,0},{8,4},{12,8},{16,12},{20,16},{24,20},{28,24},{0,28},{5,1},{9... | collective-permute-start | bytes 24584 | tf_op jit(solution)/shard_map/ppermute | solution.py:21
  221.3 0.0 collective-permute-start
  221.3 1.4 collective-permute-done.1
  222.7 0.2 fusion.13
  222.9 4.8 %collective-permute-done = bf16[4,1024]{1,0:T(4,128)(2,1)S(1)} collective-permute-done((bf16[4,1024]{1,0:T(4,128)(2,1)S(1)}, bf16[4,1024]{1,0:T(4,128)(2,1)S(1)}, u32[]{:S(2)}, u32[]{:S(2)}) %collective-permute-start) | collective-permute-done | bytes 8224 | tf_op jit(solution)/shard_map/ppermute | solution.py:20
  227.6 0.8 fusion.16
  (27 shorter events, 0.1 us)
Async XLA Ops:
  6.5 208.5 %copy-start = (bf16[5120,64]{0,1:T(8,128)(2,1)S(1)}, bf16[5120,64]{0,1:T(8,128)(2,1)}, u32[]{:S(2)}) copy-start(bf16[5120,64]{0,1:T(8,128)(2,1)} %param.21) | copy-start | bytes 1966084
  6.5 7.4 %copy-start.5 = (bf16[256,2560]{1,0:T(8,128)(2,1)S(1)}, bf16[256,2560]{1,0:T(8,128)(2,1)}, u32[]{:S(2)}) copy-start(bf16[256,2560]{1,0:T(8,128)(2,1)} %param.14) | copy-start | bytes 3932164
  6.5 107.7 %all-gather.2.cloned.1.call-start = ((), (), s32[]{:S(2)}) async-start(), calls=%async_computation.4 | async-start | bytes 7372800 | tf_op jit(solution)/shard_map/all_gather | solution.py:72
  9.7 21.5 %all-to-all-start = ((bf16[256,4,5,128]{0,3,2,1:T(8,128)(2,1)}), bf16[256,4,5,128]{0,3,2,1:T(8,128)(2,1)S(1)}, u32[]{:S(2)}, u32[]{:S(2)}) async-start(bf16[256,4,5,128]{0,3,2,1:T(8,128)(2,1)} %bitcast.2), calls=%async_computation | async-start | bytes 2621440 | tf_op jit(solution)/shard_map/all_to_all | solution.py:59
  31.2 20.8 %all-to-all-start.1 = ((bf16[256,4,5,128]{0,3,2,1:T(8,128)(2,1)}), bf16[256,4,5,128]{0,3,2,1:T(8,128)(2,1)S(1)}, u32[]{:S(2)}, u32[]{:S(2)}) async-start(bf16[256,4,5,128]{0,3,2,1:T(8,128)(2,1)} %bitcast.49), calls=%async_computation.1 | async-start | bytes 2621440 | tf_op jit(solution)/shard_map/all_to_all | solution.py:62
  52.0 4.4 %copy-start.4 = (bf16[256,4,5,128]{0,3,2,1:T(8,128)(2,1)}, bf16[256,4,5,128]{0,3,2,1:T(8,128)(2,1)S(1)}, u32[]{:S(2)}) copy-start(bf16[256,4,5,128]{0,3,2,1:T(8,128)(2,1)S(1)} %all-to-all-done.1) | copy-start | bytes 3932164
  52.0 21.6 %all-to-all-start.2 = ((bf16[256,4,5,128]{0,3,2,1:T(8,128)(2,1)}), bf16[256,4,5,128]{0,3,2,1:T(8,128)(2,1)}, u32[]{:S(2)}, u32[]{:S(2)}) async-start(bf16[256,4,5,128]{0,3,2,1:T(8,128)(2,1)} %bitcast.48), calls=%async_computation.2 | async-start | bytes 2621440 | tf_op jit(solution)/shard_map/all_to_all | solution.py:65
  56.3 154.6 %reduce-scatter.2.cloned.1.call-start = ((), (), s32[]{:S(2)}) async-start(), calls=%async_computation.5 | async-start | bytes 13107200 | tf_op jit(solution)/shard_map/reduce_scatter | solution.py:73
  83.5 7.4 %copy-start.1 = (f32[5,1024,1024]{1,2,0:T(8,128)}, f32[5,1024,1024]{1,2,0:T(8,128)S(1)}, u32[]{:S(2)}) copy-start(f32[5,1024,1024]{1,2,0:T(8,128)S(1)} %get-tuple-element.20) | copy-start | bytes 62914564
  83.5 7.4 %copy-start.6 = (bf16[1024,5,128]{0,2,1:T(8,128)(2,1)S(1)}, bf16[1024,5,128]{0,2,1:T(8,128)(2,1)}, u32[]{:S(2)}) copy-start(bf16[1024,5,128]{0,2,1:T(8,128)(2,1)} %squeeze.15) | copy-start | bytes 3932164
  128.1 0.9 copy-start.10
  128.1 3.5 %copy-start.9 = (s32[8,4,2]{0,2,1:T(2,128)S(1)}, s32[8,4,2]{0,2,1:T(2,128)}, u32[]{:S(2)}) copy-start(s32[8,4,2]{0,2,1:T(2,128)} %param.25) | copy-start | bytes 772
  128.1 82.8 %copy-start.2 = (bf16[256,5120]{1,0:T(8,128)(2,1)S(1)}, bf16[256,5120]{1,0:T(8,128)(2,1)}, u32[]{:S(2)}) copy-start(bf16[256,5120]{1,0:T(8,128)(2,1)} %param.16) | copy-start | bytes 7864324
  128.1 82.8 %copy-start.7 = (f32[5120]{0:T(1024)S(1)}, f32[5120]{0:T(1024)}, u32[]{:S(2)}) copy-start(f32[5120]{0:T(1024)} %param.18) | copy-start | bytes 61444
  132.2 82.8 %copy-start.11 = (f32[5120]{0:T(1024)S(1)}, f32[5120]{0:T(1024)}, u32[]{:S(2)}) copy-start(f32[5120]{0:T(1024)} %param.19) | copy-start | bytes 61444
  132.2 82.8 %copy-start.12 = (f32[5120]{0:T(1024)S(1)}, f32[5120]{0:T(1024)}, u32[]{:S(2)}) copy-start(f32[5120]{0:T(1024)} %param.20) | copy-start | bytes 61444
  210.9 2.8 %copy-start.3 = (bf16[256,5120]{1,0:T(8,128)(2,1)S(1)}, bf16[256,5120]{1,0:T(8,128)(2,1)}, u32[]{:S(2)}) copy-start(bf16[256,5120]{1,0:T(8,128)(2,1)} %reduce-scatter.2.cloned.1.call-done) | copy-start | bytes 7864324
  215.0 1.9 copy-start.8
  217.0 5.7 %collective-permute-start.1 = (bf16[4,1024]{1,0:T(4,128)(2,1)S(1)}, bf16[4,1024]{1,0:T(4,128)(2,1)S(1)}, u32[]{:S(2)}, u32[]{:S(2)}) collective-permute-start(bf16[4,1024]{1,0:T(4,128)(2,1)S(1)} %get-tuple-element.12), channel_id=1, source_target_pairs={{4,0},{8,4},{12,8},{16,12},{20,16},{24,20},{28,24},{0,28},{5,1},{9... | collective-permute-start | bytes 24584 | tf_op jit(solution)/shard_map/ppermute | solution.py:21
  221.3 6.3 %collective-permute-start = (bf16[4,1024]{1,0:T(4,128)(2,1)S(1)}, bf16[4,1024]{1,0:T(4,128)(2,1)S(1)}, u32[]{:S(2)}, u32[]{:S(2)}) collective-permute-start(bf16[4,1024]{1,0:T(4,128)(2,1)S(1)} %get-tuple-element.11), channel_id=1, source_target_pairs={{0,4},{4,8},{8,12},{12,16},{16,20},{20,24},{24,28},{28,0},{1,5},{5... | collective-permute-start | bytes 24584 | tf_op jit(solution)/shard_map/ppermute | solution.py:20
Sparse Core Ops, SparseCore 0:
  9.6 104.6 all-gather.1
  128.3 82.5 reduce-scatter.1
where the time goes:
time: 236 us; the launch traced here: 235 us
  waiting for transfers between devices  143 us (61%)
  matrix products  31 us (13%)
  local copies, waits for them, and re-layouts  19.9 us (8%)
  starting transfers between devices  16.5 us (7%)
  between operations  15.7 us (7%)
  other arithmetic  9.4 us (4%)
    reduce_scatter x1, waiting for transfers between devices, local(): lax.psum_scatter(jnp.dot(own_heads, full_columns, preferred_element_type=...  78.6 us
    all_to_all x1, waiting for transfers between devices, local(): lax.all_to_all(queries.reshape(split_shape), 'fsdp', split_axis=1, concat...  15.8 us
    all_to_all x1, waiting for transfers between devices, local(): lax.all_to_all(keys.reshape(split_shape), 'fsdp', split_axis=1, concat_ax...  14.8 us
    all_to_all x1, waiting for transfers between devices, local(): lax.all_to_all(values.reshape(split_shape), 'fsdp', split_axis=1, concat_...  14.7 us
    dot_general x1, matrix products, local(): jnp.dot(own_heads, full_columns, preferred_element_type=jnp.float32)  13.8 us
    all_gather x1, waiting for transfers between devices, local(): full_columns = lax.all_gather(out_weight, 'win', axis=1, tiled=True)  12.1 us
    dot_general x1, matrix products, softmax_block(): jnp.einsum('hqk,khd->qhd', probability, value_h, preferred_element_type=j...  11.2 us
    unnamed x29, local copies, waits for them, and re-layouts  10.1 us
  transfers between devices with their start and end apart: 7, of which 7 were waited for; matrix products, arithmetic and copies ran while one was open for 15% of the time, Pallas kernels for 0%

commit v1 on v0

--- a/solution.py
+++ b/solution.py
@@ -3,11 +3,39 @@
 import jax.numpy as jnp
 from jax import lax
 from jax.sharding import PartitionSpec as P
+from jax.lax import axis_index, axis_size, ppermute
 
 HEADS = 20
 HD = 128
 FD = 4
 EPSILON = 0.001
+
+
+def unite_slabs(content, where_dim):
+    content = jnp.moveaxis(content, 0, where_dim)
+    tmp = content.shape
+    return content.reshape(
+        *tmp[:where_dim], tmp[where_dim] * tmp[where_dim + 1], *tmp[where_dim + 2 :]
+    )
+
+
+def axis_part_save(u_in, dev_axis):
+    how_many = axis_size(dev_axis)
+    work_now = u_in[None]
+    for ii in range(how_many.bit_length() - 1):
+        answer = 1 << ii
+        t1 = map(lambda dev_i: (dev_i, dev_i ^ answer), range(how_many))
+        near = list(t1)
+        even = ppermute(work_now, axis_name=dev_axis, perm=near)
+        block_now = jnp.stack([work_now, even])
+        q_next = axis_index(dev_axis) >> ii & 1
+        work_now = jnp.where(q_next == 0, block_now, block_now[::-1]).reshape(-1, *u_in.shape)
+    return work_now
+
+
+def use_hubs_here(in_array, body, in_dim=1):
+    v1 = axis_part_save(in_array, body)
+    return unite_slabs(v1, in_dim)
 
 
 def padded_2(value, sides, width):
@@ -69,7 +97,7 @@
     own_heads = result.astype(jnp.bfloat16)[:, None]
     window_rows = own_heads.shape[0]
     own_heads = own_heads.reshape(window_rows, per_group * HD)
-    full_columns = lax.all_gather(out_weight, "win", axis=1, tiled=True)
+    full_columns = use_hubs_here(out_weight, "win")
     projected = lax.psum_scatter(
         jnp.dot(own_heads, full_columns, preferred_element_type=jnp.float32).astype(jnp.bfloat16),
         "fsdp",

time: 236 us -> 358 us (1.52)
  waiting for transfers between devices: 143 us -> 233 us
  local copies, waits for them, and re-layouts: 19.9 us -> 34 us
  other arithmetic: 9.4 us -> 21.6 us
  starting transfers between devices: 16.5 us -> 24.5 us
    ppermute x0 -> x3, waiting for transfers between devices: none -> 115 us  [axis_part_save(): even = ppermute(work_now, axis_name=dev_axis, perm=near)]
    all_gather x1 -> x0, waiting for transfers between devices: 12.1 us -> none  [local(): full_columns = lax.all_gather(out_weight, 'win', axis=1, tiled=True)]
    another operation x0 -> x4, other arithmetic: none -> 8.49 us  [axis_part_save(): block_now = jnp.stack([work_now, even])]
    ppermute x0 -> x3, starting transfers between devices: none -> 7.37 us  [axis_part_save(): even = ppermute(work_now, axis_name=dev_axis, perm=near)]
    all_to_all x1, waiting for transfers between devices: 14.8 us -> 7.64 us  [local(): lax.all_to_all(keys.reshape(split_shape), 'fsdp', split_axis=1, concat_ax...]
    all_to_all x1, waiting for transfers between devices: 15.8 us -> 9.38 us  [local(): lax.all_to_all(queries.reshape(split_shape), 'fsdp', split_axis=1, concat...]
    reshape x0 -> x1, local copies, waits for them, and re-layouts: none -> 5.86 us  [axis_part_save(): jnp.where(q_next == 0, block_now, block_now[::-1]).reshape(-1, *u_in.shape)]
    another operation x0 -> x1, local copies, waits for them, and re-layouts: none -> 5.68 us  [axis_part_save(): block_now = jnp.stack([work_now, even])]
  transfers between devices with their start and end apart: 7 -> 9, of which waited for: 7 -> 8; matrix products, arithmetic and copies ran while one was open for 15% -> 12% of each run, Pallas kernels for 0% -> 0%
where the time goes in v1:
time: 358 us; the launch traced here: 357 us
  waiting for transfers between devices  233 us (65%)
  local copies, waits for them, and re-layouts  34 us (9%)
  matrix products  28 us (8%)
  starting transfers between devices  24.5 us (7%)
  other arithmetic  21.6 us (6%)
  between operations  15.7 us (4%)
    ppermute x3, waiting for transfers between devices, axis_part_save(): even = ppermute(work_now, axis_name=dev_axis, perm=near)  115 us
    reduce_scatter x1, waiting for transfers between devices, local(): lax.psum_scatter(jnp.dot(own_heads, full_columns, preferred_element_type=...  81.4 us
    all_to_all x1, waiting for transfers between devices, local(): lax.all_to_all(values.reshape(split_shape), 'fsdp', split_axis=1, concat_...  13.5 us
    dot_general x1, matrix products, local(): jnp.dot(own_heads, full_columns, preferred_element_type=jnp.float32)  11.1 us
    dot_general x1, matrix products, softmax_block(): jnp.einsum('hqk,khd->qhd', probability, value_h, preferred_element_type=j...  10.9 us
    unnamed x33, local copies, waits for them, and re-layouts  10.2 us
    all_to_all x1, waiting for transfers between devices, local(): lax.all_to_all(queries.reshape(split_shape), 'fsdp', split_axis=1, concat...  9.38 us
    another operation x4, other arithmetic, axis_part_save(): block_now = jnp.stack([work_now, even])  8.49 us
  transfers between devices with their start and end apart: 9, of which 8 were waited for; matrix products, arithmetic and copies ran while one was open for 12% of the time, Pallas kernels for 0%

profile of v1, /device:TPU:0, one launch (start us, length us, event | category | flops | bytes accessed | tf_op | source)
XLA Modules:
  0.0 357.1 jit_solution(2007542536591520311)
XLA Ops:
  6.5 2.6 copy.22
  9.1 4.3 %all-to-all-start.2 = ((bf16[256,4,5,128]{0,3,2,1:T(8,128)(2,1)}), bf16[256,4,5,128]{0,3,2,1:T(8,128)(2,1)S(1)}, u32[]{:S(2)}, u32[]{:S(2)}) async-start(bf16[256,4,5,128]{0,3,2,1:T(8,128)(2,1)} %bitcast.10), calls=%async_computation.2 | async-start | bytes 2621440 | tf_op jit(solution)/shard_map/all_to_all | solution.py:93
  13.4 2.3 collective-permute-start
  15.7 1.5 copy.18
  17.1 13.5 %all-to-all-done.2 = bf16[256,4,5,128]{0,3,2,1:T(8,128)(2,1)S(1)} async-done(((bf16[256,4,5,128]{0,3,2,1:T(8,128)(2,1)}), bf16[256,4,5,128]{0,3,2,1:T(8,128)(2,1)S(1)}, u32[]{:S(2)}, u32[]{:S(2)}) %all-to-all-start.2) | async-done | bytes 1310752 | tf_op jit(solution)/shard_map/all_to_all | solution.py:93
  30.6 4.3 %all-to-all-start = ((bf16[256,4,5,128]{0,3,2,1:T(8,128)(2,1)}), bf16[256,4,5,128]{0,3,2,1:T(8,128)(2,1)}, u32[]{:S(2)}, u32[]{:S(2)}) async-start(bf16[256,4,5,128]{0,3,2,1:T(8,128)(2,1)} %bitcast.2), calls=%async_computation | async-start | bytes 2621440 | tf_op jit(solution)/shard_map/all_to_all | solution.py:87
  34.9 1.6 pad_maximum_fusion.2
  36.5 1.6 fusion.12
  38.1 2.3 collective-permute-start.1
  40.4 2.5 copy.20
  42.8 9.4 %all-to-all-done = bf16[256,4,5,128]{0,3,2,1:T(8,128)(2,1)} async-done(((bf16[256,4,5,128]{0,3,2,1:T(8,128)(2,1)}), bf16[256,4,5,128]{0,3,2,1:T(8,128)(2,1)}, u32[]{:S(2)}, u32[]{:S(2)}) %all-to-all-start) | async-done | bytes 1310752 | tf_op jit(solution)/shard_map/all_to_all | solution.py:87
  52.2 4.3 %all-to-all-start.1 = ((bf16[256,4,5,128]{0,3,2,1:T(8,128)(2,1)}), bf16[256,4,5,128]{0,3,2,1:T(8,128)(2,1)}, u32[]{:S(2)}, u32[]{:S(2)}) async-start(bf16[256,4,5,128]{0,3,2,1:T(8,128)(2,1)} %bitcast.66), calls=%async_computation.1 | async-start | bytes 2621440 | tf_op jit(solution)/shard_map/all_to_all | solution.py:90
  56.5 0.0 reduce-scatter.2.cloned.1.call-start
  56.6 3.5 copy.23
  60.1 3.7 %squeeze.15 = bf16[1024,5,128]{0,2,1:T(8,128)(2,1)} reshape(bf16[4,256,1,5,128]{1,0,4,3,2:T(4,128)(2,1)} %copy.23) | data formatting | bytes 2621440 | tf_op jit(solution)/shard_map/squeeze | solution.py:96
  63.7 2.5 copy.19
  66.2 7.6 %all-to-all-done.1 = bf16[256,4,5,128]{0,3,2,1:T(8,128)(2,1)} async-done(((bf16[256,4,5,128]{0,3,2,1:T(8,128)(2,1)}), bf16[256,4,5,128]{0,3,2,1:T(8,128)(2,1)}, u32[]{:S(2)}, u32[]{:S(2)}) %all-to-all-start.1) | async-done | bytes 1310752 | tf_op jit(solution)/shard_map/all_to_all | solution.py:90
  73.8 2.4 copy.21
  76.2 0.8 collective-permute-done.1
  77.1 1.8 pad_maximum_fusion.1
  78.8 2.4 reverse_select_fusion.1
  81.2 5.9 %copy.25 = bf16[4,640,640]{1,2,0:T(8,128)(2,1)} copy(bf16[4,640,640]{2,1,0:T(8,128)(2,1)} %bitcast.60) | data formatting | bytes 6553600 | tf_op jit(solution)/shard_map/reshape | solution.py:32
  87.1 2.8 collective-permute-start.2
  89.9 2.9 multiply_reduce_fusion
  92.8 3.7 %fusion = f32[5,1024]{1,0:T(8,128)S(1)} fusion(f32[5,1024,1024]{1,2,0:T(8,128)S(1)} %get-tuple-element.22, f32[5,1024]{1,0:T(8,128)S(1)} %get-tuple-element.21), kind=kLoop, calls=%fused_computation.2 | loop fusion | flops 15723520 | bytes 21012480 | tf_op jit(solution)/shard_map/reduce_sum | solution.py:60
  96.5 3.7 %copy-done.1 = f32[5,1024,1024]{1,2,0:T(8,128)} copy-done((f32[5,1024,1024]{1,2,0:T(8,128)}, f32[5,1024,1024]{1,2,0:T(8,128)S(1)}, u32[]{:S(2)}) %copy-start.1) | copy-done | bytes 20971544
  100.1 10.9 %fusion.7 = bf16[1024,5,128]{0,2,1:T(8,128)(2,1)S(1)} fusion(bf16[1024,5,128]{0,2,1:T(8,128)(2,1)S(1)} %copy-done.8, f32[5,1024,1024]{1,2,0:T(8,128)} %copy-done.1, f32[5,1024]{1,0:T(8,128)S(1)} %get-tuple-element.21, f32[1024,5]{0,1:T(8,128)S(1)} %bitcast.69), kind=kOutput, calls=%fused_computation.17 | convolution fusion | flops 1359216640 | bytes 23633920 | tf_op jit(solution)/shard_map/hqk,khd->qhd/dot_general | solution.py:62
  111.1 5.7 %copy.26 = bf16[1,4,640,640]{2,3,1,0:T(8,128)(2,1)} copy(bf16[1,4,640,640]{3,2,1,0:T(8,128)(2,1)} %bitcast.61) | data formatting | bytes 6553600 | tf_op jit(solution)/shard_map/stack;reshape | solution.py:30
  116.8 114.4 %collective-permute-done.2 = bf16[4,640,640]{1,2,0:T(8,128)(2,1)} collective-permute-done((bf16[4,640,640]{1,2,0:T(8,128)(2,1)}, bf16[4,640,640]{1,2,0:T(8,128)(2,1)}, u32[]{:S(2)}, u32[]{:S(2)}) %collective-permute-start.2) | collective-permute-done | bytes 3276832 | tf_op jit(solution)/shard_map/ppermute | solution.py:29
  231.2 3.6 %pad_maximum_fusion = bf16[2,4,640,640]{2,3,1,0:T(8,128)(2,1)S(1)} fusion(bf16[1,4,640,640]{2,3,1,0:T(8,128)(2,1)} %bitcast.24, bf16[1,4,640,640]{2,3,1,0:T(8,128)(2,1)} %copy.26), kind=kLoop, calls=%fused_computation.9 | loop fusion | flops 3276800 | bytes 13107200 | tf_op jit(solution)/shard_map/stack | solution.py:30
  234.8 1.3 reverse_select_fusion
  236.1 11.1 %convolution_convert_fusion = bf16[1024,5120]{1,0:T(8,128)(2,1)} fusion(bf16[1024,640]{0,1:T(8,128)(2,1)S(1)} %bitcast.70, bf16[640,5120]{0,1:T(8,128)(2,1)S(1)} %bitcast.62), kind=kOutput, calls=%fused_computation.8 | convolution fusion | flops 6716129280 | bytes 18350080 | tf_op jit(solution)/shard_map/dot_general | solution.py:102
  248.1 0.7 select_reduce_fusion.3
  250.0 0.6 iota_compare_fusion.8
  250.6 0.2 select_reduce_fusion.1
  250.8 0.2 fusion.20
  251.1 0.2 fusion.21
  251.3 81.4 %reduce-scatter.2.cloned.1.call-done = bf16[256,5120]{1,0:T(8,128)(2,1)} async-done(((bf16[1024,5120]{1,0:T(8,128)(2,1)}), bf16[256,5120]{1,0:T(8,128)(2,1)}) %reduce-scatter.2.cloned.1.call-update) | async-done | bytes 2621456 | tf_op jit(solution)/shard_map/reduce_scatter | solution.py:101
  332.6 2.8 fusion.6
  335.5 1.3 multiply_reduce_fusion.1
  336.8 1.7 fusion.19
  338.5 0.1 copy.27
  338.6 0.1 mul.85
  338.8 4.3 %collective-permute-start.4 = (bf16[4,1024]{1,0:T(4,128)(2,1)S(1)}, bf16[4,1024]{1,0:T(4,128)(2,1)S(1)}, u32[]{:S(2)}, u32[]{:S(2)}) collective-permute-start(bf16[4,1024]{1,0:T(4,128)(2,1)S(1)} %get-tuple-element.14), channel_id=1, source_target_pairs={{4,0},{8,4},{12,8},{16,12},{20,16},{24,20},{28,24},{0,28},{5,1},{9... | collective-permute-start | bytes 24584 | tf_op jit(solution)/shard_map/ppermute | solution.py:49
  343.0 1.4 collective-permute-done.4
  344.4 0.2 fusion.15
  344.6 4.8 %collective-permute-done.3 = bf16[4,1024]{1,0:T(4,128)(2,1)S(1)} collective-permute-done((bf16[4,1024]{1,0:T(4,128)(2,1)S(1)}, bf16[4,1024]{1,0:T(4,128)(2,1)S(1)}, u32[]{:S(2)}, u32[]{:S(2)}) %collective-permute-start.3) | collective-permute-done | bytes 8224 | tf_op jit(solution)/shard_map/ppermute | solution.py:48
  349.4 0.8 fusion.18
  (42 shorter events, 0.2 us)
Async XLA Ops:
  6.5 330.3 %copy-start = (bf16[5120,64]{0,1:T(8,128)(2,1)S(1)}, bf16[5120,64]{0,1:T(8,128)(2,1)}, u32[]{:S(2)}) copy-start(bf16[5120,64]{0,1:T(8,128)(2,1)} %param.21) | copy-start | bytes 1966084
  6.5 9.2 %copy-start.7 = (bf16[256,2560]{1,0:T(8,128)(2,1)S(1)}, bf16[256,2560]{1,0:T(8,128)(2,1)}, u32[]{:S(2)}) copy-start(bf16[256,2560]{1,0:T(8,128)(2,1)} %param.13) | copy-start | bytes 3932164
  9.1 21.5 %all-to-all-start.2 = ((bf16[256,4,5,128]{0,3,2,1:T(8,128)(2,1)}), bf16[256,4,5,128]{0,3,2,1:T(8,128)(2,1)S(1)}, u32[]{:S(2)}, u32[]{:S(2)}) async-start(bf16[256,4,5,128]{0,3,2,1:T(8,128)(2,1)} %bitcast.10), calls=%async_computation.2 | async-start | bytes 2621440 | tf_op jit(solution)/shard_map/all_to_all | solution.py:93
  13.4 21.5 %collective-permute-start = (bf16[1,640,640]{2,1,0:T(8,128)(2,1)}, bf16[1,640,640]{2,1,0:T(8,128)(2,1)}, u32[]{:S(2)}, u32[]{:S(2)}) collective-permute-start(bf16[1,640,640]{2,1,0:T(8,128)(2,1)} %bitcast.67), channel_id=1, source_target_pairs={{0,4},{4,0},{8,12},{12,8},{16,20},{20,16},{24,28},{28,24},{1,5},{5... | collective-permute-start | bytes 2457608 | tf_op jit(solution)/shard_map/ppermute | solution.py:29
  30.6 4.3 %copy-start.6 = (bf16[256,4,5,128]{0,3,2,1:T(8,128)(2,1)}, bf16[256,4,5,128]{0,3,2,1:T(8,128)(2,1)S(1)}, u32[]{:S(2)}) copy-start(bf16[256,4,5,128]{0,3,2,1:T(8,128)(2,1)S(1)} %all-to-all-done.2) | copy-start | bytes 3932164
  30.6 21.6 %all-to-all-start = ((bf16[256,4,5,128]{0,3,2,1:T(8,128)(2,1)}), bf16[256,4,5,128]{0,3,2,1:T(8,128)(2,1)}, u32[]{:S(2)}, u32[]{:S(2)}) async-start(bf16[256,4,5,128]{0,3,2,1:T(8,128)(2,1)} %bitcast.2), calls=%async_computation | async-start | bytes 2621440 | tf_op jit(solution)/shard_map/all_to_all | solution.py:87
  38.1 39.0 %collective-permute-start.1 = (bf16[2,640,640]{2,1,0:T(8,128)(2,1)}, bf16[2,640,640]{2,1,0:T(8,128)(2,1)}, u32[]{:S(2)}, u32[]{:S(2)}) collective-permute-start(bf16[2,640,640]{2,1,0:T(8,128)(2,1)} %get-tuple-element.12), channel_id=1, source_target_pairs={{0,8},{4,12},{8,0},{12,4},{16,24},{20,28},{24,16},{28,20},{1,9},{5... | collective-permute-start | bytes 4915208 | tf_op jit(solution)/shard_map/ppermute | solution.py:29
  52.2 21.6 %all-to-all-start.1 = ((bf16[256,4,5,128]{0,3,2,1:T(8,128)(2,1)}), bf16[256,4,5,128]{0,3,2,1:T(8,128)(2,1)}, u32[]{:S(2)}, u32[]{:S(2)}) async-start(bf16[256,4,5,128]{0,3,2,1:T(8,128)(2,1)} %bitcast.66), calls=%async_computation.1 | async-start | bytes 2621440 | tf_op jit(solution)/shard_map/all_to_all | solution.py:90
  56.5 276.1 %reduce-scatter.2.cloned.1.call-start = ((), (), s32[]{:S(2)}) async-start(), calls=%async_computation.4 | async-start | bytes 13107200 | tf_op jit(solution)/shard_map/reduce_scatter | solution.py:101
  81.2 8.6 %copy-start.4 = (bf16[4,256,1,5,128]{4,1,0,3,2:T(8,128)(2,1)S(1)}, bf16[4,256,1,5,128]{4,1,0,3,2:T(8,128)(2,1)}, u32[]{:S(2)}) copy-start(bf16[4,256,1,5,128]{4,1,0,3,2:T(8,128)(2,1)} %copy.19) | copy-start | bytes 3932164
  81.2 8.6 %copy-start.5 = (bf16[4,256,1,5,128]{4,1,0,3,2:T(8,128)(2,1)S(1)}, bf16[4,256,1,5,128]{4,1,0,3,2:T(8,128)(2,1)}, u32[]{:S(2)}) copy-start(bf16[4,256,1,5,128]{4,1,0,3,2:T(8,128)(2,1)} %copy.21) | copy-start | bytes 3932164
  87.1 144.1 %collective-permute-start.2 = (bf16[4,640,640]{1,2,0:T(8,128)(2,1)}, bf16[4,640,640]{1,2,0:T(8,128)(2,1)}, u32[]{:S(2)}, u32[]{:S(2)}) collective-permute-start(bf16[4,640,640]{1,2,0:T(8,128)(2,1)} %copy.25), channel_id=1, source_target_pairs={{0,16},{4,20},{8,24},{12,28},{16,0},{20,4},{24,8},{28,12},{1,17},{... | collective-permute-start | bytes 9830408 | tf_op jit(solution)/shard_map/ppermute | solution.py:29
  92.8 7.4 %copy-start.1 = (f32[5,1024,1024]{1,2,0:T(8,128)}, f32[5,1024,1024]{1,2,0:T(8,128)S(1)}, u32[]{:S(2)}) copy-start(f32[5,1024,1024]{1,2,0:T(8,128)S(1)} %get-tuple-element.22) | copy-start | bytes 62914564
  92.8 7.4 %copy-start.8 = (bf16[1024,5,128]{0,2,1:T(8,128)(2,1)S(1)}, bf16[1024,5,128]{0,2,1:T(8,128)(2,1)}, u32[]{:S(2)}) copy-start(bf16[1024,5,128]{0,2,1:T(8,128)(2,1)} %squeeze.15) | copy-start | bytes 3932164
  247.2 0.8 copy-start.12
  247.2 3.4 copy-start.11
  247.2 85.4 %copy-start.2 = (bf16[256,5120]{1,0:T(8,128)(2,1)S(1)}, bf16[256,5120]{1,0:T(8,128)(2,1)}, u32[]{:S(2)}) copy-start(bf16[256,5120]{1,0:T(8,128)(2,1)} %param.16) | copy-start | bytes 7864324
  247.2 85.4 %copy-start.9 = (f32[5120]{0:T(1024)S(1)}, f32[5120]{0:T(1024)}, u32[]{:S(2)}) copy-start(f32[5120]{0:T(1024)} %param.18) | copy-start | bytes 61444
  332.6 2.9 copy-start.3
  335.5 1.3 copy-start.13
  335.5 1.3 copy-start.14
  336.8 1.9 copy-start.10
  338.8 5.6 %collective-permute-start.4 = (bf16[4,1024]{1,0:T(4,128)(2,1)S(1)}, bf16[4,1024]{1,0:T(4,128)(2,1)S(1)}, u32[]{:S(2)}, u32[]{:S(2)}) collective-permute-start(bf16[4,1024]{1,0:T(4,128)(2,1)S(1)} %get-tuple-element.14), channel_id=1, source_target_pairs={{4,0},{8,4},{12,8},{16,12},{20,16},{24,20},{28,24},{0,28},{5,1},{9... | collective-permute-start | bytes 24584 | tf_op jit(solution)/shard_map/ppermute | solution.py:49
  343.0 6.3 %collective-permute-start.3 = (bf16[4,1024]{1,0:T(4,128)(2,1)S(1)}, bf16[4,1024]{1,0:T(4,128)(2,1)S(1)}, u32[]{:S(2)}, u32[]{:S(2)}) collective-permute-start(bf16[4,1024]{1,0:T(4,128)(2,1)S(1)} %get-tuple-element.13), channel_id=1, source_target_pairs={{0,4},{4,8},{8,12},{12,16},{16,20},{20,24},{24,28},{28,0},{1,5},{5... | collective-permute-start | bytes 24584 | tf_op jit(solution)/shard_map/ppermute | solution.py:48
Sparse Core Ops, SparseCore 0:
  247.4 85.2 reduce-scatter.1
